TPU v7x, 128 devices: a whole 4x4x4 slice. The times are simulated.
128 devices in a mesh: rep: 4 (over x_hi, core), tp: 32 (over z, x_lo, y).
Axes of the slice: x: 4 (x_hi: 2, x_lo: 2; x = x_hi * 2 + x_lo), y: 4, z: 4, core: 2. Of those that a mesh axis runs over, the one named last changes fastest.
Arguments:
- trainer_query: float32 [128, 64, 8192], P(('rep', 'tp')), may hold values from -6 to 6
- trainer_output: float32 [128, 8192, 64], P(('rep', 'tp')), may hold values from -6 to 6
- probes: bfloat16 [768, 8192], replicated, may hold values from -0.0625 to 0.0625
- shard_block: int32 [128], replicated, may hold values from 0 to 127, each once
- slice_owner: int32 [32], replicated, may hold values from 0 to 31, each once
Outputs:
- query_slices: bfloat16 [32, 8192, 256], P('tp')
- output_slices: bfloat16 [32, 256, 8192], P('tp')
- query_prints: float32 [32, 768, 256], P('tp')
- output_prints: float32 [32, 256, 768], P('tp')
Inputs may be any that keep to these rules, and one draw needn't show every extreme that they name: `shard_block`: a permutation: each number once. `slice_owner`: a permutation: each number once.
All inputs are finite; a program needn't handle non-finite values.
Results may differ from a plain program's by a relative error of at most 0.0029.
Values may be sent and summed in bfloat16 or wider, within the bound.
A program may use at most 128 MiB of HBM per device.

v0:
```python
import jax
import jax.numpy as jnp
from jax import lax
from jax.sharding import PartitionSpec as P


def cut_along(shard, dim, length):
    dims = shard.shape
    pieces = shard.reshape(*dims[:dim], length, dims[dim] // length, *dims[dim + 1 :])
    return jnp.moveaxis(pieces, dim, 0)


def edges_of(length, count):
    unit = 8 if length >= 8 * count else 1
    return [length // unit * k // count * unit for k in range(1, count)]


def laid_out(pieces, dim):
    pieces = jnp.moveaxis(pieces, 0, dim)
    dims = pieces.shape
    return pieces.reshape(*dims[:dim], dims[dim] * dims[dim + 1], *dims[dim + 2 :])


def cut_exchange(shard, axis, pieces, split_dim, concat_dim):
    blocks = cut_along(shard, split_dim, lax.axis_size(axis))
    split_at = max(range(1, max(2, blocks.ndim - 1)), key=lambda d: blocks.shape[d])
    outs = []
    for section in jnp.split(blocks, edges_of(blocks.shape[split_at], pieces), axis=split_at):
        if section.size:
            outs.append(lax.all_to_all(section, axis, split_axis=0, concat_axis=0, tiled=True))
    return laid_out(jnp.concatenate(outs, axis=split_at), concat_dim)


def per_device(trainer_query, trainer_output, probes, shard_block, slice_owner):
    tp_count = lax.axis_size("tp")
    rep_count = lax.axis_size("rep")
    dev_count = tp_count * rep_count
    shard_rows = trainer_query.shape[1]
    query_width = trainer_query.shape[2]
    slice_width = query_width // tp_count
    model_width = shard_rows * dev_count
    positions = jnp.arange(dev_count, dtype=jnp.int32)
    inverse = jnp.zeros((dev_count,), jnp.int32).at[shard_block].set(positions)
    query_local = trainer_query[0].astype(jnp.bfloat16)
    query_blocks = jnp.take(
        query_local.reshape(shard_rows, tp_count, slice_width), slice_owner, axis=1
    ).reshape(shard_rows, query_width)
    output_local = trainer_output[0].astype(jnp.bfloat16)
    output_blocks = jnp.take(
        output_local.reshape(tp_count, slice_width, shard_rows), slice_owner, axis=0
    ).reshape(query_width, shard_rows)
    query_moved = lax.all_to_all(query_blocks, "tp", split_axis=1, concat_axis=0, tiled=True)
    query_all = lax.all_gather(query_moved, "rep", axis=0, tiled=True)
    output_moved = cut_exchange(output_blocks, "tp", 2, 0, 1)
    output_all = lax.all_gather(output_moved, "rep", axis=1, tiled=True)
    query_ordered = query_all.reshape(dev_count, shard_rows, slice_width)
    query_slice = jnp.take(query_ordered, inverse, axis=0).reshape(model_width, slice_width)
    output_ordered = output_all.reshape(slice_width, dev_count, shard_rows)
    output_slice = jnp.take(output_ordered, inverse, axis=1).reshape(slice_width, model_width)
    query_prints = jnp.dot(probes, query_slice, preferred_element_type=jnp.float32)
    output_prints = lax.dot_general(
        output_slice, probes, (((1,), (1,)), ((), ())), preferred_element_type=jnp.float32
    )
    return (query_slice[None], output_slice[None], query_prints[None], output_prints[None])


def solution(mesh):
    placed = (P(("rep", "tp"), None, None), P(("rep", "tp"), None, None), P(), P(), P())
    return jax.shard_map(
        per_device,
        mesh=mesh,
        in_specs=placed,
        out_specs=(
            P("tp", None, None),
            P("tp", None, None),
            P("tp", None, None),
            P("tp", None, None),
        ),
        check_vma=False,
    )
```

profile of v0, /device:TPU:1, one launch (start us, length us, event | category | flops | bytes accessed | tf_op | source)
XLA Modules:
  0.0 165.8 jit_solution(11763954619681203649)
XLA Ops:
  7.2 0.7 compare_select_fusion
  7.9 0.7 compare_and_fusion
  8.5 1.7 %convert_element_type.16 = bf16[1,8192,64]{1,2,0:T(8,128)(2,1)S(1)} convert(f32[1,8192,64]{1,2,0:T(8,128)} %param.6) | non-fusion elementwise | flops 524288 | bytes 3145728 | tf_op jit(solution)/shard_map/convert_element_type | solution.py:48
  10.5 0.6 copy.13
  11.1 0.6 gather_fusion.2
  12.2 19.7 %all_to_all.26 = bf16[32,128,64]{1,2,0:T(8,128)(2,1)S(1)} all-to-all(bf16[32,128,64]{1,2,0:T(8,128)(2,1)S(1)} %get-tuple-element.16), channel_id=1, replica_groups=mesh['rep'=4,'tp'=32] {'tp'}, dimensions={0} | all-to-all | bytes 1048576 | tf_op jit(solution)/shard_map/all_to_all | solution.py:30
  31.9 15.4 %all_to_all.27 = bf16[32,128,64]{1,2,0:T(8,128)(2,1)S(1)} all-to-all(bf16[32,128,64]{1,2,0:T(8,128)(2,1)S(1)} %get-tuple-element.17), channel_id=1, replica_groups=mesh['rep'=4,'tp'=32] {'tp'}, dimensions={0} | all-to-all | bytes 1048576 | tf_op jit(solution)/shard_map/all_to_all | solution.py:30
  47.2 1.1 pad_maximum_fusion
  48.8 0.6 copy.12
  49.4 0.6 gather_fusion
  50.2 27.8 %all_to_all.28 = bf16[64,32,256]{2,0,1:T(8,128)(2,1)} all-to-all(bf16[64,32,256]{2,0,1:T(8,128)(2,1)S(1)} %select_bitcast_fusion), channel_id=1, replica_groups=mesh['rep'=4,'tp'=32] {'tp'}, dimensions={1} | all-to-all | bytes 2097152 | tf_op jit(solution)/shard_map/all_to_all | solution.py:52
  78.1 1.2 scatter_custom_fusion
  79.5 15.6 %all-gather.5.cloned.1.call-done = bf16[256,8192]{0,1:T(8,128)(2,1)} async-done(((bf16[256,2048]{0,1:T(8,128)(2,1)}), bf16[256,8192]{0,1:T(8,128)(2,1)}) %all-gather.5.cloned.1.call-update) | async-done | bytes 4194320 | tf_op jit(solution)/shard_map/all_gather | solution.py:55
  95.1 5.0 %gather_fusion.3 = bf16[128,256,64]{1,2,0:T(8,128)(2,1)} fusion(bf16[256,128,64]{0,2,1:T(8,128)(2,1)} %bitcast.43, s32[1024]{0:T(1024)S(1)} %pad_clamp_fusion), kind=kCustom, calls=%fused_computation.3 | custom fusion | bytes 8389120 | tf_op jit(solution)/shard_map/jit(_take)/gather | solution.py:59
  100.1 5.3 %bitcast_select_fusion.1 = bf16[1,256,8192]{1,2,0:T(8,128)(2,1)} fusion(pred[8192]{0:T(1024)(128)(4,1)S(1)} %broadcast_in_dim.67, bf16[1,256,8192]{1,2,0:T(8,128)(2,1)} %bitcast.41), kind=kLoop, calls=%fused_computation.6 | loop fusion | flops 2097152 | bytes 8396800 | tf_op jit(solution)/shard_map/jit(_take)/select_n | solution.py:59
  105.3 6.5 %copy.14 = bf16[1,256,8192]{2,1,0:T(8,128)(2,1)} copy(bf16[1,256,8192]{1,2,0:T(8,128)(2,1)} %bitcast_select_fusion.1) | data formatting | bytes 8388608
  111.8 6.0 %bitcast_select_fusion = bf16[256,8192]{0,1:T(8,128)(2,1)S(1)} fusion(bf16[128,256,64]{1,2,0:T(8,128)(2,1)} %gather_fusion.3, pred[8192]{0:T(1024)(128)(4,1)S(1)} %broadcast_in_dim.67), kind=kLoop, calls=%fused_computation.5 | loop fusion | flops 2097152 | bytes 8396800 | tf_op jit(solution)/shard_map/jit(_take)/select_n | solution.py:59
  117.8 7.4 %convolution_bitcast_fusion = f32[1,256,768]{2,1,0:T(8,128)} fusion(bf16[256,8192]{0,1:T(8,128)(2,1)S(1)} %bitcast_select_fusion, bf16[768,8192]{1,0:T(8,128)(2,1)} %param.7), kind=kOutput, calls=%fused_computation.9 | convolution fusion | flops 3221225472 | bytes 17563648 | tf_op jit(solution)/shard_map/dot_general | solution.py:61
  125.2 9.8 %all-gather.3.cloned.1.call-done = bf16[8192,256]{1,0:T(8,128)(2,1)} async-done(((bf16[2048,256]{1,0:T(8,128)(2,1)}), bf16[8192,256]{1,0:T(8,128)(2,1)}) %all-gather.3.cloned.1.call-update) | async-done | bytes 4194320 | tf_op jit(solution)/shard_map/all_gather | solution.py:53
  135.0 5.0 %gather_fusion.1 = bf16[128,64,256]{2,1,0:T(8,128)(2,1)} fusion(bf16[128,64,256]{2,1,0:T(8,128)(2,1)} %bitcast.46, s32[1024]{0:T(1024)S(1)} %pad_clamp_fusion), kind=kCustom, calls=%fused_computation.1 | custom fusion | bytes 8389120 | tf_op jit(solution)/shard_map/jit(_take)/gather | solution.py:57
  140.1 6.0 %bitcast_select_fusion.2 = bf16[8192,256]{1,0:T(8,128)(2,1)S(1)} fusion(bf16[128,64,256]{2,1,0:T(8,128)(2,1)} %gather_fusion.1, pred[8192]{0:T(1024)(128)(4,1)S(1)} %broadcast_in_dim.67), kind=kLoop, calls=%fused_computation.7 | loop fusion | flops 2097152 | bytes 8396800 | tf_op jit(solution)/shard_map/jit(_take)/select_n | solution.py:57
  146.0 6.5 %convolution_bitcast_fusion.1 = f32[1,768,256]{1,2,0:T(8,128)S(1)} fusion(bf16[8192,256]{1,0:T(8,128)(2,1)S(1)} %bitcast_select_fusion.2, bf16[768,8192]{1,0:T(8,128)(2,1)} %param.7), kind=kOutput, calls=%fused_computation.10 | convolution fusion | flops 3221225472 | bytes 17563648 | tf_op jit(solution)/shard_map/dot_general | solution.py:60
  152.6 1.1 copy.15
  153.7 5.2 %bitcast_select_fusion.3 = bf16[1,8192,256]{2,1,0:T(8,128)(2,1)} fusion(pred[8192]{0:T(1024)(128)(4,1)S(1)} %broadcast_in_dim.67, bf16[1,8192,256]{2,1,0:T(8,128)(2,1)} %bitcast.42), kind=kLoop, calls=%fused_computation.8 | loop fusion | flops 2097152 | bytes 8396800 | tf_op jit(solution)/shard_map/jit(_take)/select_n | solution.py:57
  (22 shorter events, 1.6 us)
Async XLA Ops:
  7.2 87.9 %all-gather.5.cloned.1.call-start = ((), (), s32[]{:S(2)}) async-start(), calls=%async_computation.4 | async-start | bytes 5242880 | tf_op jit(solution)/shard_map/all_gather | solution.py:55
  11.9 36.5 %copy-start = (f32[1,64,8192]{2,1,0:T(8,128)S(1)}, f32[1,64,8192]{2,1,0:T(8,128)}, u32[]{:S(2)}) copy-start(f32[1,64,8192]{2,1,0:T(8,128)} %param.5) | copy-start | bytes 6291460
  48.4 86.7 %all-gather.3.cloned.1.call-start = ((), (), s32[]{:S(2)}) async-start(), calls=%async_computation.3 | async-start | bytes 5242880 | tf_op jit(solution)/shard_map/all_gather | solution.py:53
  49.4 28.7 %copy-start.1 = (s32[128]{0:T(128)S(1)}, s32[128]{0:T(128)}, u32[]{:S(2)}) copy-start(s32[128]{0:T(128)} %param.8) | copy-start | bytes 1540
Sparse Core Ops, SparseCore 0:
  48.5 46.5 all-gather.4
  96.7 38.2 all-gather.2
where the time goes:
time: 167 us; the launch traced here: 166 us
  blocking collectives  62.9 us (38%)
  other arithmetic  27 us (16%)
  waiting for transfers between devices  25.4 us (15%)
  local copies, waits for them, and re-layouts  22.2 us (13%)
  between operations  14.2 us (9%)
  matrix products  13.9 us (8%)
    all_to_all x2, blocking collectives, cut_exchange(): lax.all_to_all(section, axis, split_axis=0, concat_axis=0, tiled=True)  35 us
    all_to_all x1, blocking collectives, per_device(): lax.all_to_all(query_blocks, 'tp', split_axis=1, concat_axis=0, tiled=True)  27.8 us
    all_gather x1, waiting for transfers between devices, per_device(): output_all = lax.all_gather(output_moved, 'rep', axis=1, tiled=True)  15.6 us
    select_n x2, other arithmetic, per_device(): jnp.take(output_ordered, inverse, axis=1).reshape(slice_width, model_width)  11.2 us
    select_n x3, other arithmetic, per_device(): jnp.take(query_ordered, inverse, axis=0).reshape(model_width, slice_width)  11.2 us
    all_gather x1, waiting for transfers between devices, per_device(): query_all = lax.all_gather(query_moved, 'rep', axis=0, tiled=True)  9.84 us
    unnamed x8, local copies, waits for them, and re-layouts  8.14 us
    dot_general x1, matrix products, per_device(): lax.dot_general(output_slice, probes, (((1,), (1,)), ((), ())), preferred...  7.43 us
  transfers between devices with their start and end apart: 2, of which 2 were waited for; matrix products, arithmetic and copies ran while one was open for 20% of the time, Pallas kernels for 0%

commit v1 on v0

--- a/solution.py
+++ b/solution.py
@@ -52,7 +52,9 @@
     query_moved = lax.all_to_all(query_blocks, "tp", split_axis=1, concat_axis=0, tiled=True)
     query_all = lax.all_gather(query_moved, "rep", axis=0, tiled=True)
     output_moved = cut_exchange(output_blocks, "tp", 2, 0, 1)
-    output_all = lax.all_gather(output_moved, "rep", axis=1, tiled=True)
+    output_all = jnp.concatenate(
+        lax.all_to_all(jnp.stack([output_moved] * lax.axis_size("rep")), "rep", 0, 0), axis=1
+    )
     query_ordered = query_all.reshape(dev_count, shard_rows, slice_width)
     query_slice = jnp.take(query_ordered, inverse, axis=0).reshape(model_width, slice_width)
     output_ordered = output_all.reshape(slice_width, dev_count, shard_rows)

time: 167 us -> 212 us (1.27)
  waiting for transfers between devices: 25.4 us -> 90.9 us
  blocking collectives: 62.9 us -> 19.6 us
  starting transfers between devices: 0.08 us -> 18.8 us
  local copies, waits for them, and re-layouts: 22.2 us -> 25.2 us
    all_to_all x0 -> x3, waiting for transfers between devices: none -> 90.2 us  [the longest x1 69.1 us: per_device(): lax.all_to_all(jnp.stack([output_moved] * lax.axis_size('rep')), 'rep', 0...]
    all_to_all x1 -> x0, blocking collectives: 27.8 us -> none  [per_device(): lax.all_to_all(query_blocks, 'tp', split_axis=1, concat_axis=0, tiled=True)]
    all_to_all x0 -> x3, starting transfers between devices: none -> 18.8 us  [the longest x1 6.92 us: per_device(): lax.all_to_all(jnp.stack([output_moved] * lax.axis_size('rep')), 'rep', 0...]
    all_gather x1 -> x0, waiting for transfers between devices: 15.6 us -> none  [per_device(): output_all = lax.all_gather(output_moved, 'rep', axis=1, tiled=True)]
    all_to_all x2 -> x1, blocking collectives: 35 us -> 19.6 us  [cut_exchange(): lax.all_to_all(section, axis, split_axis=0, concat_axis=0, tiled=True)]
    all_gather x1, waiting for transfers between devices: 9.84 us -> 0.01 us  [per_device(): query_all = lax.all_gather(query_moved, 'rep', axis=0, tiled=True)]
    another operation x0 -> x1, local copies, waits for them, and re-layouts: none -> 2.36 us  [per_device(): jnp.stack([output_moved] * lax.axis_size('rep'))]
    unnamed x8 -> x12, local copies, waits for them, and re-layouts: 8.14 us -> 7.99 us
  transfers between devices with their start and end apart: 2 -> 4, of which waited for: 2 -> 3; matrix products, arithmetic and copies ran while one was open for 20% -> 17% of each run, Pallas kernels for 0% -> 0%
where the time goes in v1:
time: 212 us; the launch traced here: 211 us
  waiting for transfers between devices  90.9 us (43%)
  other arithmetic  28.1 us (13%)
  local copies, waits for them, and re-layouts  25.2 us (12%)
  blocking collectives  19.6 us (9%)
  starting transfers between devices  18.8 us (9%)
  between operations  14.2 us (7%)
  matrix products  13.9 us (7%)
    all_to_all x1, waiting for transfers between devices, per_device(): lax.all_to_all(jnp.stack([output_moved] * lax.axis_size('rep')), 'rep', 0...  69.1 us
    all_to_all x1, blocking collectives, cut_exchange(): lax.all_to_all(section, axis, split_axis=0, concat_axis=0, tiled=True)  19.6 us
    all_to_all x1, waiting for transfers between devices, per_device(): lax.all_to_all(query_blocks, 'tp', split_axis=1, concat_axis=0, tiled=True)  14.1 us
    select_n x2, other arithmetic, per_device(): jnp.take(output_ordered, inverse, axis=1).reshape(slice_width, model_width)  11.2 us
    select_n x3, other arithmetic, per_device(): jnp.take(query_ordered, inverse, axis=0).reshape(model_width, slice_width)  11.2 us
    unnamed x12, local copies, waits for them, and re-layouts  7.99 us
    dot_general x1, matrix products, per_device(): lax.dot_general(output_slice, probes, (((1,), (1,)), ((), ())), preferred...  7.38 us
    all_to_all x1, waiting for transfers between devices, cut_exchange(): lax.all_to_all(section, axis, split_axis=0, concat_axis=0, tiled=True)  6.98 us
  transfers between devices with their start and end apart: 4, of which 3 were waited for; matrix products, arithmetic and copies ran while one was open for 17% of the time, Pallas kernels for 0%

profile of v1, /device:TPU:1, one launch (start us, length us, event | category | flops | bytes accessed | tf_op | source)
XLA Modules:
  0.0 210.8 jit_solution(13686621969802074042)
XLA Ops:
  8.5 1.7 convert_element_type.16
  11.9 1.1 fusion.2
  13.0 19.6 %all_to_all.31 = bf16[32,128,64]{1,2,0:T(8,128)(2,1)} all-to-all(bf16[32,128,64]{1,2,0:T(8,128)(2,1)S(1)} %get-tuple-element.16), channel_id=1, replica_groups=mesh['rep'=4,'tp'=32] {'tp'}, dimensions={0} | all-to-all | bytes 1048576 | tf_op jit(solution)/shard_map/all_to_all | solution.py:30
  32.6 5.9 %all-to-all-start.2 = ((bf16[32,128,64]{1,2,0:T(8,128)(2,1)}), bf16[32,128,64]{1,2,0:T(8,128)(2,1)}, u32[]{:S(2)}, u32[]{:S(2)}) async-start(bf16[32,128,64]{1,2,0:T(8,128)(2,1)} %get-tuple-element.17), calls=%async_computation.2 | async-start | bytes 1048576 | tf_op jit(solution)/shard_map/all_to_all | solution.py:30
  40.2 1.1 select_bitcast_fusion
  41.3 7.0 %all-to-all-done.2 = bf16[32,128,64]{1,2,0:T(8,128)(2,1)} async-done(((bf16[32,128,64]{1,2,0:T(8,128)(2,1)}), bf16[32,128,64]{1,2,0:T(8,128)(2,1)}, u32[]{:S(2)}, u32[]{:S(2)}) %all-to-all-start.2) | async-done | bytes 524320 | tf_op jit(solution)/shard_map/all_to_all | solution.py:30
  48.3 5.9 %all-to-all-start = ((bf16[64,32,256]{2,0,1:T(8,128)(2,1)}), bf16[64,32,256]{2,0,1:T(8,128)(2,1)S(1)}, u32[]{:S(2)}, u32[]{:S(2)}) async-start(bf16[64,32,256]{2,0,1:T(8,128)(2,1)} %select_bitcast_fusion), calls=%async_computation | async-start | bytes 2097152 | tf_op jit(solution)/shard_map/all_to_all | solution.py:52
  54.2 1.2 pad_maximum_fusion
  55.4 14.1 %all-to-all-done = bf16[64,32,256]{2,0,1:T(8,128)(2,1)S(1)} async-done(((bf16[64,32,256]{2,0,1:T(8,128)(2,1)}), bf16[64,32,256]{2,0,1:T(8,128)(2,1)S(1)}, u32[]{:S(2)}, u32[]{:S(2)}) %all-to-all-start) | async-done | bytes 1048608 | tf_op jit(solution)/shard_map/all_to_all | solution.py:52
  69.6 2.4 %stack.3 = bf16[4,256,2048]{1,2,0:T(8,128)(2,1)} broadcast(bf16[256,2048]{0,1:T(8,128)(2,1)S(1)} %bitcast.45), dimensions={1,2} | broadcast | bytes 5242880 | tf_op jit(solution)/shard_map/stack | solution.py:56
  71.9 6.9 %all-to-all-start.3 = ((bf16[4,256,2048]{1,2,0:T(8,128)(2,1)}), bf16[4,256,2048]{1,2,0:T(8,128)(2,1)}, u32[]{:S(2)}, u32[]{:S(2)}) async-start(bf16[4,256,2048]{1,2,0:T(8,128)(2,1)} %stack.3), calls=%async_computation.3 | async-start | bytes 8388608 | tf_op jit(solution)/shard_map/all_to_all | solution.py:56
  78.9 0.7 all-gather.2.cloned.1.call-update
  79.6 1.2 scatter_custom_fusion
  81.0 69.1 %all-to-all-done.3 = bf16[4,256,2048]{1,2,0:T(8,128)(2,1)} async-done(((bf16[4,256,2048]{1,2,0:T(8,128)(2,1)}), bf16[4,256,2048]{1,2,0:T(8,128)(2,1)}, u32[]{:S(2)}, u32[]{:S(2)}) %all-to-all-start.3) | async-done | bytes 4194336 | tf_op jit(solution)/shard_map/all_to_all | solution.py:56
  150.1 5.0 %gather_fusion.3 = bf16[128,256,64]{1,2,0:T(8,128)(2,1)} fusion(bf16[256,128,64]{0,2,1:T(8,128)(2,1)} %bitcast.8, s32[1024]{0:T(1024)S(1)} %pad_clamp_fusion), kind=kCustom, calls=%fused_computation.3 | custom fusion | bytes 8389120 | tf_op jit(solution)/shard_map/jit(_take)/gather | solution.py:61
  155.1 5.3 %bitcast_select_fusion.1 = bf16[1,256,8192]{1,2,0:T(8,128)(2,1)} fusion(pred[8192]{0:T(1024)(128)(4,1)S(1)} %broadcast_in_dim.67, bf16[1,256,8192]{1,2,0:T(8,128)(2,1)} %bitcast.43), kind=kLoop, calls=%fused_computation.6 | loop fusion | flops 2097152 | bytes 8396800 | tf_op jit(solution)/shard_map/jit(_take)/select_n | solution.py:61
  160.4 6.3 %copy.14 = bf16[1,256,8192]{2,1,0:T(8,128)(2,1)} copy(bf16[1,256,8192]{1,2,0:T(8,128)(2,1)} %bitcast_select_fusion.1) | data formatting | bytes 8388608
  166.7 6.0 %bitcast_select_fusion = bf16[256,8192]{0,1:T(8,128)(2,1)S(1)} fusion(bf16[128,256,64]{1,2,0:T(8,128)(2,1)} %gather_fusion.3, pred[8192]{0:T(1024)(128)(4,1)S(1)} %broadcast_in_dim.67), kind=kLoop, calls=%fused_computation.5 | loop fusion | flops 2097152 | bytes 8396800 | tf_op jit(solution)/shard_map/jit(_take)/select_n | solution.py:61
  172.7 7.4 %convolution_bitcast_fusion = f32[1,256,768]{2,1,0:T(8,128)} fusion(bf16[256,8192]{0,1:T(8,128)(2,1)S(1)} %bitcast_select_fusion, bf16[768,8192]{1,0:T(8,128)(2,1)} %param.7), kind=kOutput, calls=%fused_computation.9 | convolution fusion | flops 3221225472 | bytes 17563648 | tf_op jit(solution)/shard_map/dot_general | solution.py:63
  180.1 5.0 %gather_fusion.1 = bf16[128,64,256]{2,1,0:T(8,128)(2,1)} fusion(bf16[128,64,256]{2,1,0:T(8,128)(2,1)} %bitcast.48, s32[1024]{0:T(1024)S(1)} %pad_clamp_fusion), kind=kCustom, calls=%fused_computation.1 | custom fusion | bytes 8389120 | tf_op jit(solution)/shard_map/jit(_take)/gather | solution.py:59
  185.1 6.0 %bitcast_select_fusion.2 = bf16[8192,256]{1,0:T(8,128)(2,1)S(1)} fusion(bf16[128,64,256]{2,1,0:T(8,128)(2,1)} %gather_fusion.1, pred[8192]{0:T(1024)(128)(4,1)S(1)} %broadcast_in_dim.67), kind=kLoop, calls=%fused_computation.7 | loop fusion | flops 2097152 | bytes 8396800 | tf_op jit(solution)/shard_map/jit(_take)/select_n | solution.py:59
  191.0 6.5 %convolution_bitcast_fusion.1 = f32[1,768,256]{1,2,0:T(8,128)S(1)} fusion(bf16[8192,256]{1,0:T(8,128)(2,1)S(1)} %bitcast_select_fusion.2, bf16[768,8192]{1,0:T(8,128)(2,1)} %param.7), kind=kOutput, calls=%fused_computation.10 | convolution fusion | flops 3221225472 | bytes 17563648 | tf_op jit(solution)/shard_map/dot_general | solution.py:62
  197.6 1.1 copy.15
  198.7 5.2 %bitcast_select_fusion.3 = bf16[1,8192,256]{2,1,0:T(8,128)(2,1)} fusion(pred[8192]{0:T(1024)(128)(4,1)S(1)} %broadcast_in_dim.67, bf16[1,8192,256]{2,1,0:T(8,128)(2,1)} %bitcast.44), kind=kLoop, calls=%fused_computation.8 | loop fusion | flops 2097152 | bytes 8396800 | tf_op jit(solution)/shard_map/jit(_take)/select_n | solution.py:59
  (28 shorter events, 4.7 us)
Async XLA Ops:
  11.7 26.9 %copy-start.1 = (f32[1,64,8192]{2,1,0:T(8,128)S(1)}, f32[1,64,8192]{2,1,0:T(8,128)}, u32[]{:S(2)}) copy-start(f32[1,64,8192]{2,1,0:T(8,128)} %param.5) | copy-start | bytes 6291460
  32.6 15.7 %all-to-all-start.2 = ((bf16[32,128,64]{1,2,0:T(8,128)(2,1)}), bf16[32,128,64]{1,2,0:T(8,128)(2,1)}, u32[]{:S(2)}, u32[]{:S(2)}) async-start(bf16[32,128,64]{1,2,0:T(8,128)(2,1)} %get-tuple-element.17), calls=%async_computation.2 | async-start | bytes 1048576 | tf_op jit(solution)/shard_map/all_to_all | solution.py:30
  38.9 15.3 %copy-start.2 = (bf16[32,128,64]{1,2,0:T(8,128)(2,1)S(1)}, bf16[32,128,64]{1,2,0:T(8,128)(2,1)}, u32[]{:S(2)}) copy-start(bf16[32,128,64]{1,2,0:T(8,128)(2,1)} %all_to_all.31) | copy-start | bytes 1572868
  48.3 21.3 %all-to-all-start = ((bf16[64,32,256]{2,0,1:T(8,128)(2,1)}), bf16[64,32,256]{2,0,1:T(8,128)(2,1)S(1)}, u32[]{:S(2)}, u32[]{:S(2)}) async-start(bf16[64,32,256]{2,0,1:T(8,128)(2,1)} %select_bitcast_fusion), calls=%async_computation | async-start | bytes 2097152 | tf_op jit(solution)/shard_map/all_to_all | solution.py:52
  69.6 2.4 %copy-start = (bf16[64,32,256]{2,0,1:T(8,128)(2,1)}, bf16[64,32,256]{2,0,1:T(8,128)(2,1)S(1)}, u32[]{:S(2)}) copy-start(bf16[64,32,256]{2,0,1:T(8,128)(2,1)S(1)} %all-to-all-done) | copy-start | bytes 3145732
  71.9 7.6 %copy-start.3 = (s32[128]{0:T(128)S(1)}, s32[128]{0:T(128)}, u32[]{:S(2)}) copy-start(s32[128]{0:T(128)} %param.8) | copy-start | bytes 1540
  71.9 78.2 %all-to-all-start.3 = ((bf16[4,256,2048]{1,2,0:T(8,128)(2,1)}), bf16[4,256,2048]{1,2,0:T(8,128)(2,1)}, u32[]{:S(2)}, u32[]{:S(2)}) async-start(bf16[4,256,2048]{1,2,0:T(8,128)(2,1)} %stack.3), calls=%async_computation.3 | async-start | bytes 8388608 | tf_op jit(solution)/shard_map/all_to_all | solution.py:56
  78.8 101.2 %all-gather.2.cloned.1.call-start = ((), (), s32[]{:S(2)}) async-start(), calls=%async_computation.4 | async-start | bytes 5242880 | tf_op jit(solution)/shard_map/all_gather | solution.py:53
Sparse Core Ops, SparseCore 0:
  81.3 60.5 all-gather.1
